TPU v7x, 32 devices: a whole 2x2x4 slice. The times are simulated.
32 devices in a mesh: mem: 4 (over y, x), tile: 8 (over z, core).
Axes of the slice: x: 2, y: 2, z: 4, core: 2. Of those that a mesh axis runs over, the one named last changes fastest.
Arguments:
- ensemble: float32 [1024, 3, 64, 256], P('mem', None, 'tile'), may hold values from -4.5 to 5
- obs_cells: int32 [8, 256], replicated, may hold values from 0 to 6143
- region_tile: int32 [8], replicated, may hold values from 0 to 7, each once
- obs_values: float32 [8, 256], replicated, may hold values from -5.6 to 5.6
- obs_error: float32 [8, 256], replicated, may hold values from 0.05 to 0.75
Outputs:
- analysis: float32 [1024, 3, 64, 256], P('mem', None, 'tile')
Inputs may be any that keep to these rules, and one draw needn't show every extreme that they name: `obs_cells`: row r lists flat indices into the values of tile region_tile[r], ordered by field, then row within the tile, then column; indices may repeat. `region_tile`: each tile holds exactly one region.
All inputs are finite; a program needn't handle non-finite values.
Results may differ from a plain program's by a relative error of at most 0.00029.
Values sent between devices are 32-bit elements; how exact they have to be, the bound alone decides.
No kernel may reach another device: no remote copies, remote signals or barrier semaphores. Data moves between devices by JAX's collectives and lax.ppermute only.
A program may use at most 128 MiB of HBM per device.

v0:
```python
import math
import jax
import jax.numpy as jnp
from jax import lax
from jax.sharding import PartitionSpec as P

ENSEMBLE_SIZE = 1024
STEPS = 4
DEGREE = 4
DEPTH = 1.0
GRAVITY = 1.0
CORIOLIS = 0.5
TIMESTEP = 0.3
DIFFUSE = 0.1
PRECISE = lax.Precision.HIGHEST


def with_halo(cells, sides, width):
    for axis, dim in sides:
        count = lax.axis_size(axis)
        head = lax.slice_in_dim(cells, 0, width, axis=dim)
        tail = lax.slice_in_dim(cells, cells.shape[dim] - width, cells.shape[dim], axis=dim)
        cells = jnp.concatenate(
            [
                lax.ppermute(tail, axis, [(i, (i + 1) % count) for i in range(count)]),
                cells,
                lax.ppermute(head, axis, [((i + 1) % count, i) for i in range(count)]),
            ],
            axis=dim,
        )
    return cells


def east_diff(quantity):
    return 0.5 * (jnp.roll(quantity, -1, axis=-1) - jnp.roll(quantity, 1, axis=-1))


def north_diff(quantity):
    return 0.5 * (quantity[:, 2:] - quantity[:, :-2])


def interior(quantity):
    return quantity[:, 1:-1]


def smoothing(quantity):
    middle = interior(quantity)
    return (
        jnp.roll(middle, -1, axis=-1)
        + jnp.roll(middle, 1, axis=-1)
        + quantity[:, 2:]
        + quantity[:, :-2]
        - 4.0 * middle
    )


def advance(padded):
    height = padded[:, 0]
    eastward = padded[:, 1]
    northward = padded[:, 2]
    height_mid = interior(height)
    east_mid = interior(eastward)
    north_mid = interior(northward)
    column = DEPTH + height
    height_rate = -(interior(east_diff(column * eastward)) + north_diff(column * northward))
    east_rate = (
        -(east_mid * interior(east_diff(eastward)) + north_mid * north_diff(eastward))
        - GRAVITY * interior(east_diff(height))
        + CORIOLIS * north_mid
    )
    north_rate = (
        -(east_mid * interior(east_diff(northward)) + north_mid * north_diff(northward))
        - GRAVITY * north_diff(height)
        - CORIOLIS * east_mid
    )
    return jnp.stack(
        [
            height_mid + TIMESTEP * height_rate + DIFFUSE * smoothing(height),
            east_mid + TIMESTEP * east_rate + DIFFUSE * smoothing(eastward),
            north_mid + TIMESTEP * north_rate + DIFFUSE * smoothing(northward),
        ],
        axis=1,
    )


def innovations(observed, target, variance, weight):
    obs_mean = jnp.mean(observed, axis=0)
    perturbed = (observed - obs_mean) * weight
    misfit = (target - obs_mean) * weight
    spread = jnp.sum(perturbed * perturbed, axis=0) / (observed.shape[0] - 1)
    return (perturbed, misfit, jnp.sum(misfit * misfit), jnp.sum(weight * (spread + variance)))


def gram_terms(perturbed, misfit, variance):
    weighted_matrix = perturbed / variance
    product = jnp.einsum("mo,no->mn", weighted_matrix, perturbed, precision=PRECISE)
    projected = jnp.dot(perturbed, misfit / variance, precision=PRECISE)
    return (product, projected)


def spectral_map(gram_scaled):
    upper_bound = 2.0 + jnp.sqrt(jnp.sum(gram_scaled * gram_scaled))
    order_count = gram_scaled.shape[0]
    shifted = 2.0 / (upper_bound - 1.0) * gram_scaled - jnp.eye(order_count, dtype=jnp.float32)
    orders = jnp.arange(DEGREE + 1, dtype=jnp.float32)
    angles = (orders + 0.5) * (math.pi / (DEGREE + 1))
    levels = 0.5 * (upper_bound + 1.0) + 0.5 * (upper_bound - 1.0) * jnp.cos(angles)
    values = lax.rsqrt(levels)
    cos_table = jnp.cos(orders[:, None] * angles[None, :])
    coeffs = 2.0 / (DEGREE + 1) * jnp.sum(cos_table * values[None, :], axis=1)
    coeffs = coeffs * jnp.where(orders == 0.0, 0.5, 1.0)
    return (shifted, coeffs)


def chebyshev(shifted, operand, coeffs):
    previous = operand
    current = jnp.dot(shifted, operand, precision=PRECISE)
    summed = coeffs[0] * previous + coeffs[1] * current
    for term_index in range(2, DEGREE + 1):
        following = 2.0 * jnp.dot(shifted, current, precision=PRECISE) - previous
        summed = summed + coeffs[term_index] * following
        previous, current = (current, following)
    return summed


def analyse(columns, product, projected, inflation):
    gram_scaled = inflation / (ENSEMBLE_SIZE - 1) * product
    shifted, coeffs = spectral_map(gram_scaled)
    centre = jnp.mean(columns, axis=0)
    spread = columns - centre
    shaped = chebyshev(shifted, spread, coeffs)
    weights = (
        inflation
        / (ENSEMBLE_SIZE - 1)
        * chebyshev(shifted, chebyshev(shifted, projected, coeffs), coeffs)
    )
    mean_shift = jnp.dot(weights, spread, precision=PRECISE)
    return centre + jnp.sqrt(inflation) * shaped + mean_shift


def on_device(ensemble, obs_cells, region_tile, obs_values, obs_error):
    layered_arrays = ensemble
    for repeat in range(STEPS):
        layered_arrays = advance(with_halo(layered_arrays, (("tile", 2),), 1))
    chosen = (region_tile == lax.axis_index("tile"))[:, None]
    obs_index = jnp.sum(jnp.where(chosen, obs_cells, 0), axis=0)
    target = jnp.sum(jnp.where(chosen, obs_values, 0.0), axis=0)
    variance = jnp.sum(jnp.where(chosen, obs_error, 0.0), axis=0)
    flat_state = layered_arrays.reshape(layered_arrays.shape[0], -1)
    columns = lax.all_to_all(flat_state, "mem", split_axis=1, concat_axis=0, tiled=True)
    selected_entries = jnp.take(flat_state, obs_index, axis=1)
    observed = lax.all_gather(selected_entries, "mem", axis=0, tiled=True)
    unit = jnp.ones(target.shape, jnp.float32)
    perturbed, misfit, misfit_sum, spread_sum = innovations(observed, target, variance, unit)
    misfit_sum, spread_sum = lax.psum((misfit_sum, spread_sum), "tile")
    product, projected = gram_terms(perturbed, misfit, variance)
    inflation = misfit_sum / spread_sum
    updated = analyse(columns, product, projected, inflation)
    restored_fields = lax.all_to_all(updated, "mem", split_axis=0, concat_axis=1, tiled=True)
    return restored_fields.reshape(ensemble.shape)


def solution(mesh):
    in_specs = (P("mem", None, "tile", None), P(), P(), P(), P())
    out_specs = P("mem", None, "tile", None)
    return jax.shard_map(
        on_device, mesh=mesh, in_specs=in_specs, out_specs=out_specs, check_vma=False
    )
```

profile of v0, /device:TPU:0, one launch (start us, length us, event | category | flops | bytes accessed | tf_op | source)
XLA Modules:
  0.0 589.1 jit_solution(11982423487698862288)
XLA Ops:
  6.5 6.6 %copy.15 = f32[256,3,8,256]{0,3,2,1:T(8,128)} copy(f32[256,3,8,256]{3,2,1,0:T(8,128)} %param.5) | data formatting | bytes 12582912 | tf_op args[0]
  15.1 4.1 collective-permute-start.1
  19.2 15.4 %collective-permute-done = f32[256,3,1,256]{0,3,2,1:T(8,128)S(1)} collective-permute-done((f32[256,3,1,256]{0,3,2,1:T(8,128)S(1)}, f32[256,3,1,256]{0,3,2,1:T(8,128)S(1)}, u32[]{:S(2)}, u32[]{:S(2)}) %collective-permute-start) | collective-permute-done | bytes 786464 | tf_op jit(solution)/shard_map/ppermute | solution.py:25
  35.1 3.2 pad_maximum_fusion
  47.9 3.5 fusion.248
  51.4 3.5 fusion.254
  54.9 4.9 fusion.110
  59.9 3.8 fusion.130
  65.0 4.6 fusion.118
  74.2 14.4 %collective-permute-done.2 = f32[256,3,1,256]{0,3,2,1:T(8,128)S(1)} collective-permute-done((f32[256,3,1,256]{0,3,2,1:T(8,128)S(1)}, f32[256,3,1,256]{0,3,2,1:T(8,128)S(1)}, u32[]{:S(2)}, u32[]{:S(2)}) %collective-permute-start.2) | collective-permute-done | bytes 786464 | tf_op jit(solution)/shard_map/ppermute | solution.py:25
  104.6 4.6 fusion.77
  109.3 4.2 fusion.97
  113.4 5.6 fusion.85
  124.8 14.8 %collective-permute-done.4 = f32[256,3,1,256]{0,3,2,1:T(8,128)S(1)} collective-permute-done((f32[256,3,1,256]{0,3,2,1:T(8,128)}, f32[256,3,1,256]{0,3,2,1:T(8,128)S(1)}, u32[]{:S(2)}, u32[]{:S(2)}) %collective-permute-start.4) | collective-permute-done | bytes 786464 | tf_op jit(solution)/shard_map/ppermute | solution.py:25
  157.1 4.6 fusion.44
  161.7 3.8 fusion.64
  165.5 4.6 fusion.52
  175.1 13.7 %collective-permute-done.6 = f32[256,3,1,256]{0,3,2,1:T(8,128)S(1)} collective-permute-done((f32[256,3,1,256]{0,3,2,1:T(8,128)S(1)}, f32[256,3,1,256]{0,3,2,1:T(8,128)S(1)}, u32[]{:S(2)}, u32[]{:S(2)}) %collective-permute-start.6) | collective-permute-done | bytes 786464 | tf_op jit(solution)/shard_map/ppermute | solution.py:25
  200.8 5.3 fusion.11
  206.1 4.0 fusion.31
  210.1 3.4 fusion.19
  213.5 3.3 pad_maximum_fusion.4
  216.8 3.8 gather_fusion
  221.5 5.3 all-to-all-start
  226.8 62.4 %all-gather.2.cloned.1.call-done = f32[1024,256]{0,1:T(8,128)} async-done(((f32[256,256]{0,1:T(8,128)}), f32[1024,256]{0,1:T(8,128)}) %all-gather.2.cloned.1.call-update) | async-done | bytes 1048592 | tf_op jit(solution)/shard_map/all_gather | solution.py:152
  293.4 17.0 %all-reduce = (f32[]{:T(128)}, f32[]{:T(128)}) all-reduce(f32[]{:T(128)} %get-tuple-element.150, f32[]{:T(128)} %add_reduce_fusion), channel_id=1, replica_groups=mesh['mem'=4,'tile'=8] {'tile'}, use_global_device_ids=true, to_apply=%region_5.6 | all-reduce | flops 2 | bytes 16 | tf_op jit(solution)/shard_map/psum | solution.py:155
  311.8 7.0 %multiply_reduce_fusion = (f32[]{:T(128)}, f32[1024,1024]{1,0:T(8,128)}) fusion(f32[]{:T(128)S(6)} %div.46, f32[1024,256]{0,1:T(8,128)S(1)} %copy-done.10, f32[256]{0:T(256)S(1)} %get-tuple-element.151, f32[256]{0:T(256)S(1)} %get-tuple-element.6), kind=kOutput, calls=%fused_computation.12 | convolution fusion | flops 3225157632 | bytes 5244936 | tf_op jit(solution)/shard_map/mo,no->mn/dot_general | solution.py:96
  321.1 6.2 %fusion.193 = f32[1,1024]{1,0:T(1,128)S(1)} fusion(f32[1,1024]{1,0:T(1,128)S(1)} %fusion.184, f32[1024,1024]{1,0:T(8,128)} %get-tuple-element.158, f32[]{:T(128)S(6)} %div.49, f32[]{:T(128)S(6)} %div.46), kind=kOutput, calls=%fused_computation.291 | convolution fusion | flops 17825792 | bytes 4202504 | tf_op jit(solution)/shard_map/dot_general | solution.py:117
  327.4 3.9 fusion.191
  331.3 3.9 fusion.201
  335.3 4.1 fusion.200
  339.4 3.1 multiply_add_fusion
  342.5 3.9 fusion.199
  346.4 3.9 fusion.189
  350.3 3.9 fusion.198
  354.3 4.3 fusion.197
  358.6 3.1 add_multiply_fusion.8
  361.7 3.1 reduce_sum.92
  364.9 6.6 %copy.18 = f32[4,256,1536]{2,1,0:T(8,128)} copy(f32[4,256,1536]{1,2,0:T(8,128)} %bitcast.30) | data formatting | bytes 12582912 | tf_op jit(solution)/shard_map/all_to_all | solution.py:150
  371.4 3.6 bitcast_subtract_fusion
  375.4 20.7 %fusion.203 = f32[1024,1536]{1,0:T(8,128)S(1)} fusion(f32[1024,1536]{1,0:T(8,128)S(1)} %bitcast_subtract_fusion, f32[1024,1024]{1,0:T(8,128)S(1)} %copy-done.1, f32[]{:T(128)S(6)} %div.49, f32[]{:T(128)S(6)} %div.46), kind=kOutput, calls=%fused_computation.319 | convolution fusion | flops 19332595712 | bytes 16777224 | tf_op jit(solution)/shard_map/dot_general | solution.py:117
  396.1 3.1 convolution_reduce_fusion
  399.2 21.6 %multiply_subtract_fusion.1 = f32[1024,1536]{1,0:T(8,128)S(1)} fusion(f32[1024,1536]{1,0:T(8,128)S(1)} %bitcast_subtract_fusion, f32[1024,1536]{1,0:T(8,128)S(1)} %fusion.203, f32[1024,1024]{1,0:T(8,128)S(1)} %copy-done.1, f32[]{:T(128)S(6)} %div.49, f32[]{:T(128)S(6)} %div.46), kind=kOutput, calls=%fused_computation.9 | convolution fusion | flops 19335741440 | bytes 23068680 | tf_op jit(solution)/shard_map/dot_general | solution.py:120
  423.5 22.3 %fusion.202 = f32[1024,1536]{1,0:T(8,128)} fusion(f32[1024,1536]{1,0:T(8,128)S(1)} %multiply_subtract_fusion.1, f32[1024,1024]{1,0:T(8,128)S(1)} %copy-done.1, f32[]{:T(128)S(6)} %div.49, f32[]{:T(128)S(6)} %div.46), kind=kOutput, calls=%fused_computation.318 | convolution fusion | flops 19332595712 | bytes 16777224 | tf_op jit(solution)/shard_map/dot_general | solution.py:120
  445.8 32.6 %add_add_fusion = f32[1024,1536]{1,0:T(8,128)} fusion(f32[1024,1536]{1,0:T(8,128)} %copy-done.21, f32[1024,1536]{1,0:T(8,128)} %copy-done.20, f32[1024,1536]{1,0:T(8,128)S(1)} %bitcast_subtract_fusion, f32[1024,1536]{1,0:T(8,128)} %fusion.202, f32[1536]{0:T(1024)S(1)} %convolution_reduce_fusion, f32[]{:T(128)} %bitcast.35, f32[]{:T(128)} %bitcast.34, ...), kind=kOutput, calls=%fused_computation.7 | convolution fusion | flops 19360907264 | bytes 35663904 | tf_op jit(solution)/shard_map/dot_general | solution.py:120
  478.4 88.7 %all_to_all.35 = f32[4,256,1536]{2,1,0:T(8,128)S(1)} all-to-all(f32[4,256,1536]{2,1,0:T(8,128)} %bitcast.135), channel_id=1, replica_groups=mesh['mem'=4,'tile'=8] {'mem'}, dimensions={0} | all-to-all | bytes 12582912 | tf_op jit(solution)/shard_map/all_to_all | solution.py:159
  567.1 6.7 %copy.19 = f32[256,4,1536]{2,1,0:T(4,128)} copy(f32[256,4,1536]{2,0,1:T(8,128)S(1)} %bitcast.134) | data formatting | bytes 12582912 | tf_op jit(solution)/shard_map/all_to_all | solution.py:159
  573.8 8.3 %reshape.53 = f32[256,3,8,256]{3,2,1,0:T(8,128)} reshape(f32[256,4,1536]{2,1,0:T(4,128)} %copy.19) | data formatting | bytes 12582912 | tf_op jit(solution)/shard_map/reshape | solution.py:160
  (145 shorter events, 83.6 us)
Async XLA Ops:
  6.5 282.7 %all-gather.2.cloned.1.call-start = ((), (), s32[]{:S(2)}) async-start(), calls=%async_computation.2 | async-start | bytes 1310720 | tf_op jit(solution)/shard_map/all_gather | solution.py:152
  14.6 20.1 %collective-permute-start = (f32[256,3,1,256]{0,3,2,1:T(8,128)S(1)}, f32[256,3,1,256]{0,3,2,1:T(8,128)S(1)}, u32[]{:S(2)}, u32[]{:S(2)}) collective-permute-start(f32[256,3,1,256]{0,3,2,1:T(8,128)S(1)} %get-tuple-element.35), channel_id=1, source_target_pairs={{0,1},{1,2},{2,3},{3,4},{4,5},{5,6},{6,7},{7,0},{8,9},{9,10},{10,1... | collective-permute-start | bytes 2359304 | tf_op jit(solution)/shard_map/ppermute | solution.py:25
  15.1 20.0 %collective-permute-start.1 = (f32[256,3,1,256]{0,3,2,1:T(8,128)S(1)}, f32[256,3,1,256]{0,3,2,1:T(8,128)S(1)}, u32[]{:S(2)}, u32[]{:S(2)}) collective-permute-start(f32[256,3,1,256]{0,3,2,1:T(8,128)S(1)} %get-tuple-element.36), channel_id=1, source_target_pairs={{1,0},{2,1},{3,2},{4,3},{5,4},{6,5},{7,6},{0,7},{9,8},{10,9},{11,1... | collective-permute-start | bytes 2359304 | tf_op jit(solution)/shard_map/ppermute | solution.py:27
  54.9 5.0 copy-start.9
  54.9 5.0 copy-start.14
  59.8 3.8 copy-start.4
  59.9 3.8 copy-start.5
  59.9 4.6 copy-start.6
  59.9 5.2 copy-start.13
  69.8 18.8 %collective-permute-start.2 = (f32[256,3,1,256]{0,3,2,1:T(8,128)S(1)}, f32[256,3,1,256]{0,3,2,1:T(8,128)S(1)}, u32[]{:S(2)}, u32[]{:S(2)}) collective-permute-start(f32[256,3,1,256]{0,3,2,1:T(8,128)S(1)} %get-tuple-element.33), channel_id=1, source_target_pairs={{0,1},{1,2},{2,3},{3,4},{4,5},{5,6},{6,7},{7,0},{8,9},{9,10},{10,1... | collective-permute-start | bytes 2359304 | tf_op jit(solution)/shard_map/ppermute | solution.py:25
  71.8 17.3 %collective-permute-start.3 = (f32[256,3,1,256]{0,3,2,1:T(8,128)S(1)}, f32[256,3,1,256]{0,3,2,1:T(8,128)S(1)}, u32[]{:S(2)}, u32[]{:S(2)}) collective-permute-start(f32[256,3,1,256]{0,3,2,1:T(8,128)S(1)} %get-tuple-element.34), channel_id=1, source_target_pairs={{1,0},{2,1},{3,2},{4,3},{5,4},{6,5},{7,6},{0,7},{9,8},{10,9},{11,1... | collective-permute-start | bytes 2359304 | tf_op jit(solution)/shard_map/ppermute | solution.py:27
  104.6 4.7 copy-start.7
  113.4 5.6 copy-start.2
  119.1 1.8 copy-start.3
  120.9 18.8 %collective-permute-start.4 = (f32[256,3,1,256]{0,3,2,1:T(8,128)}, f32[256,3,1,256]{0,3,2,1:T(8,128)S(1)}, u32[]{:S(2)}, u32[]{:S(2)}) collective-permute-start(f32[256,3,1,256]{0,3,2,1:T(8,128)} %get-tuple-element.31), channel_id=1, source_target_pairs={{0,1},{1,2},{2,3},{3,4},{4,5},{5,6},{6,7},{7,0},{8,9},{9,10},{10,1... | collective-permute-start | bytes 2359304 | tf_op jit(solution)/shard_map/ppermute | solution.py:25
  123.3 17.6 %collective-permute-start.5 = (f32[256,3,1,256]{0,3,2,1:T(8,128)}, f32[256,3,1,256]{0,3,2,1:T(8,128)}, u32[]{:S(2)}, u32[]{:S(2)}) collective-permute-start(f32[256,3,1,256]{0,3,2,1:T(8,128)} %get-tuple-element.32), channel_id=1, source_target_pairs={{1,0},{2,1},{3,2},{4,3},{5,4},{6,5},{7,6},{0,7},{9,8},{10,9},{11,1... | collective-permute-start | bytes 2359304 | tf_op jit(solution)/shard_map/ppermute | solution.py:27
  157.0 4.6 copy-start.8
  170.1 4.3 copy-start.19
  170.2 4.3 copy-start.17
  170.3 18.4 %collective-permute-start.6 = (f32[256,3,1,256]{0,3,2,1:T(8,128)S(1)}, f32[256,3,1,256]{0,3,2,1:T(8,128)S(1)}, u32[]{:S(2)}, u32[]{:S(2)}) collective-permute-start(f32[256,3,1,256]{0,3,2,1:T(8,128)S(1)} %get-tuple-element.29), channel_id=1, source_target_pairs={{0,1},{1,2},{2,3},{3,4},{4,5},{5,6},{6,7},{7,0},{8,9},{9,10},{10,1... | collective-permute-start | bytes 2359304 | tf_op jit(solution)/shard_map/ppermute | solution.py:25
  172.4 17.3 %collective-permute-start.7 = (f32[256,3,1,256]{0,3,2,1:T(8,128)S(1)}, f32[256,3,1,256]{0,3,2,1:T(8,128)S(1)}, u32[]{:S(2)}, u32[]{:S(2)}) collective-permute-start(f32[256,3,1,256]{0,3,2,1:T(8,128)S(1)} %get-tuple-element.30), channel_id=1, source_target_pairs={{1,0},{2,1},{3,2},{4,3},{5,4},{6,5},{7,6},{0,7},{9,8},{10,9},{11,1... | collective-permute-start | bytes 2359304 | tf_op jit(solution)/shard_map/ppermute | solution.py:27
  206.1 4.0 copy-start.11
  210.1 3.4 copy-start.12
  216.8 3.8 copy-start.18
  216.8 4.7 copy-start.15
  216.8 4.7 copy-start.16
  221.5 140.2 %all-to-all-start = ((f32[256,4,1536]{0,2,1:T(8,128)}), f32[256,4,1536]{0,2,1:T(8,128)}, u32[]{:S(2)}, u32[]{:S(2)}) async-start(f32[256,4,1536]{0,2,1:T(8,128)} %bitcast.133), calls=%async_computation | async-start | bytes 12582912 | tf_op jit(solution)/shard_map/all_to_all | solution.py:150
  289.2 22.6 %copy-start.10 = (f32[1024,256]{0,1:T(8,128)S(1)}, f32[1024,256]{0,1:T(8,128)}, u32[]{:S(2)}) copy-start(f32[1024,256]{0,1:T(8,128)} %all-gather.2.cloned.1.call-done) | copy-start | bytes 3145732
  321.1 6.3 %copy-start = (f32[1024,1024]{1,0:T(8,128)S(1)}, f32[1024,1024]{1,0:T(8,128)}, u32[]{:S(2)}) copy-start(f32[1024,1024]{1,0:T(8,128)} %get-tuple-element.158) | copy-start | bytes 12582916
  371.4 4.0 copy-start.1
  396.1 3.1 copy-start.20
  420.8 2.7 copy-start.21
Sparse Core Ops, SparseCore 0:
  221.5 67.6 all-gather.1
where the time goes:
time: 597 us; the launch traced here: 589 us
  matrix products  142 us (24%)
  waiting for transfers between devices  124 us (21%)
  blocking collectives  106 us (18%)
  local copies, waits for them, and re-layouts  90.5 us (15%)
  other arithmetic  87.9 us (15%)
  starting transfers between devices  22.3 us (4%)
  between operations  16.4 us (3%)
    dot_general x9, matrix products, chebyshev(): following = 2.0 * jnp.dot(shifted, current, precision=PRECISE) - previous  101 us
    all_to_all x1, blocking collectives, on_device(): lax.all_to_all(updated, 'mem', split_axis=0, concat_axis=1, tiled=True)  88.7 us
    all_gather x1, waiting for transfers between devices, on_device(): observed = lax.all_gather(selected_entries, 'mem', axis=0, tiled=True)  62.4 us
    ppermute x4, waiting for transfers between devices, with_halo(): lax.ppermute(tail, axis, [(i, (i + 1) % count) for i in range(count)])  58.3 us
    another operation x13, other arithmetic, advance(): jnp.stack([height_mid + TIMESTEP * height_rate + DIFFUSE * smoothing(heig...  56.7 us
    dot_general x3, matrix products, chebyshev(): current = jnp.dot(shifted, operand, precision=PRECISE)  30.8 us
    slice x22, local copies, waits for them, and re-layouts, smoothing(): jnp.roll(middle, 1, axis=-1)  25.4 us
    slice x30, local copies, waits for them, and re-layouts, east_diff(): jnp.roll(quantity, 1, axis=-1)  23.1 us
  transfers between devices with their start and end apart: 10, of which 9 were waited for; matrix products, arithmetic and copies ran while one was open for 9% of the time, Pallas kernels for 0%

commit v1 on v0

--- a/solution.py
+++ b/solution.py
@@ -149,7 +149,12 @@
     flat_state = layered_arrays.reshape(layered_arrays.shape[0], -1)
     columns = lax.all_to_all(flat_state, "mem", split_axis=1, concat_axis=0, tiled=True)
     selected_entries = jnp.take(flat_state, obs_index, axis=1)
-    observed = lax.all_gather(selected_entries, "mem", axis=0, tiled=True)
+    ring = [selected_entries]
+    for hop in range(3):
+        ring.append(lax.ppermute(ring[-1], "mem", [(dev, (dev + 1) % 4) for dev in range(4)]))
+    observed = jnp.roll(
+        jnp.concatenate(ring[::-1], axis=0), (lax.axis_index("mem") + 1) * ring[0].shape[0], axis=0
+    )
     unit = jnp.ones(target.shape, jnp.float32)
     perturbed, misfit, misfit_sum, spread_sum = innovations(observed, target, variance, unit)
     misfit_sum, spread_sum = lax.psum((misfit_sum, spread_sum), "tile")

time: 597 us -> 524 us (0.88)
  waiting for transfers between devices: 124 us -> 81 us
  blocking collectives: 106 us -> 88.6 us
  between operations: 16.4 us -> 3.07 us
    all_gather x1 -> x0, waiting for transfers between devices: 62.4 us -> none  [on_device(): observed = lax.all_gather(selected_entries, 'mem', axis=0, tiled=True)]
    ppermute x0 -> x3, waiting for transfers between devices: none -> 18.1 us  [on_device(): lax.ppermute(ring[-1], 'mem', [(dev, (dev + 1) % 4) for dev in range(4)])]
    all_to_all x1, blocking collectives: 88.7 us -> 74.3 us  [on_device(): lax.all_to_all(updated, 'mem', split_axis=0, concat_axis=1, tiled=True)]
  transfers between devices with their start and end apart: 10 -> 12, of which waited for: 9 -> 12; matrix products, arithmetic and copies ran while one was open for 9% -> 10% of each run, Pallas kernels for 0% -> 0%
where the time goes in v1:
time: 524 us; the launch traced here: 516 us
  matrix products  142 us (27%)
  local copies, waits for them, and re-layouts  90.6 us (17%)
  blocking collectives  88.6 us (17%)
  other arithmetic  84.3 us (16%)
  waiting for transfers between devices  81 us (15%)
  starting transfers between devices  26.4 us (5%)
    dot_general x9, matrix products, chebyshev(): following = 2.0 * jnp.dot(shifted, current, precision=PRECISE) - previous  101 us
    all_to_all x1, blocking collectives, on_device(): lax.all_to_all(updated, 'mem', split_axis=0, concat_axis=1, tiled=True)  74.3 us
    ppermute x4, waiting for transfers between devices, with_halo(): lax.ppermute(tail, axis, [(i, (i + 1) % count) for i in range(count)])  58.8 us
    another operation x13, other arithmetic, advance(): jnp.stack([height_mid + TIMESTEP * height_rate + DIFFUSE * smoothing(heig...  56.7 us
    dot_general x3, matrix products, chebyshev(): current = jnp.dot(shifted, operand, precision=PRECISE)  30.8 us
    slice x22, local copies, waits for them, and re-layouts, smoothing(): jnp.roll(middle, 1, axis=-1)  25.4 us
    slice x30, local copies, waits for them, and re-layouts, east_diff(): jnp.roll(quantity, 1, axis=-1)  23.1 us
    ppermute x3, waiting for transfers between devices, on_device(): lax.ppermute(ring[-1], 'mem', [(dev, (dev + 1) % 4) for dev in range(4)])  18.1 us
  transfers between devices with their start and end apart: 12, of which 12 were waited for; matrix products, arithmetic and copies ran while one was open for 10% of the time, Pallas kernels for 0%

profile of v1, /device:TPU:0, one launch (start us, length us, event | category | flops | bytes accessed | tf_op | source)
XLA Modules:
  0.0 516.4 jit_solution(7031139568421119075)
XLA Ops:
  0.0 6.6 %copy.15 = f32[256,3,8,256]{0,3,2,1:T(8,128)} copy(f32[256,3,8,256]{3,2,1,0:T(8,128)} %param.5) | data formatting | bytes 12582912 | tf_op args[0]
  8.6 4.1 collective-permute-start.1
  12.7 15.4 %collective-permute-done = f32[256,3,1,256]{0,3,2,1:T(8,128)S(1)} collective-permute-done((f32[256,3,1,256]{0,3,2,1:T(8,128)S(1)}, f32[256,3,1,256]{0,3,2,1:T(8,128)S(1)}, u32[]{:S(2)}, u32[]{:S(2)}) %collective-permute-start) | collective-permute-done | bytes 786464 | tf_op jit(solution)/shard_map/ppermute | solution.py:25
  28.6 3.2 pad_maximum_fusion
  41.3 3.5 fusion.248
  44.9 3.5 fusion.254
  48.3 4.9 fusion.110
  53.3 3.8 fusion.130
  58.5 4.6 fusion.118
  67.6 14.4 %collective-permute-done.2 = f32[256,3,1,256]{0,3,2,1:T(8,128)S(1)} collective-permute-done((f32[256,3,1,256]{0,3,2,1:T(8,128)S(1)}, f32[256,3,1,256]{0,3,2,1:T(8,128)S(1)}, u32[]{:S(2)}, u32[]{:S(2)}) %collective-permute-start.2) | collective-permute-done | bytes 786464 | tf_op jit(solution)/shard_map/ppermute | solution.py:25
  98.1 4.6 fusion.77
  102.7 4.2 fusion.97
  106.9 5.6 %fusion.85 = f32[256,1,8,256]{0,3,2,1:T(8,128)S(1)} fusion(f32[256,10,1]{0,2,1:T(1,128)S(1)} %get-tuple-element.110, f32[256,10,255]{0,2,1:T(8,128)S(1)} %get-tuple-element.112, f32[256,10,255]{0,2,1:T(8,128)S(1)} %get-tuple-element.111, f32[256,10,1]{0,2,1:T(1,128)S(1)} %get-tuple-element.109, f32[256,10,1]{0,2,1:T(1,128)S(1)} %get-tuple-element.106, ...), kind=kLoop, calls=%fused_computation.139 | loop fusion | flops 14680064 | bytes 25165824 | tf_op jit(solution)/shard_map/stack | solution.py:76
  118.3 14.8 %collective-permute-done.4 = f32[256,3,1,256]{0,3,2,1:T(8,128)S(1)} collective-permute-done((f32[256,3,1,256]{0,3,2,1:T(8,128)}, f32[256,3,1,256]{0,3,2,1:T(8,128)S(1)}, u32[]{:S(2)}, u32[]{:S(2)}) %collective-permute-start.4) | collective-permute-done | bytes 786464 | tf_op jit(solution)/shard_map/ppermute | solution.py:25
  150.5 4.6 fusion.44
  155.1 3.8 fusion.64
  159.0 4.6 fusion.52
  168.0 14.1 %collective-permute-done.6 = f32[256,3,1,256]{0,3,2,1:T(8,128)S(1)} collective-permute-done((f32[256,3,1,256]{0,3,2,1:T(8,128)S(1)}, f32[256,3,1,256]{0,3,2,1:T(8,128)S(1)}, u32[]{:S(2)}, u32[]{:S(2)}) %collective-permute-start.6) | collective-permute-done | bytes 786464 | tf_op jit(solution)/shard_map/ppermute | solution.py:25
  194.2 5.3 %fusion.11 = f32[256,1,8,256]{0,3,2,1:T(8,128)} fusion(f32[256,10,1]{0,2,1:T(1,128)S(1)} %get-tuple-element.62, f32[256,10,255]{0,2,1:T(8,128)S(1)} %get-tuple-element.64, f32[256,10,255]{0,2,1:T(8,128)S(1)} %get-tuple-element.63, f32[256,10,1]{0,2,1:T(1,128)S(1)} %get-tuple-element.61, f32[256,8,1]{0,2,1:T(1,128)S(1)} %get-tuple-element.58, ...), kind=kLoop, calls=%fused_computation.45 | loop fusion | flops 13631488 | bytes 24117248 | tf_op jit(solution)/shard_map/stack | solution.py:76
  199.6 4.0 fusion.31
  203.6 3.4 fusion.19
  207.0 3.3 pad_maximum_fusion.4
  210.3 3.8 gather_fusion
  216.2 6.6 %collective-permute-done.8 = f32[256,256]{0,1:T(8,128)S(1)} collective-permute-done((f32[256,256]{0,1:T(8,128)S(1)}, f32[256,256]{0,1:T(8,128)S(1)}, u32[]{:S(2)}, u32[]{:S(2)}) %collective-permute-start.8) | collective-permute-done | bytes 262176 | tf_op jit(solution)/shard_map/ppermute | solution.py:154
  224.1 8.3 %collective-permute-done.9 = f32[256,256]{0,1:T(8,128)S(1)} collective-permute-done((f32[256,256]{0,1:T(8,128)S(1)}, f32[256,256]{0,1:T(8,128)S(1)}, u32[]{:S(2)}, u32[]{:S(2)}) %collective-permute-start.9) | collective-permute-done | bytes 262176 | tf_op jit(solution)/shard_map/ppermute | solution.py:154
  233.2 5.3 %all-to-all-start = ((f32[256,4,1536]{0,2,1:T(8,128)}), f32[256,4,1536]{0,2,1:T(8,128)}, u32[]{:S(2)}, u32[]{:S(2)}) async-start(f32[256,4,1536]{0,2,1:T(8,128)} %bitcast.137), calls=%async_computation | async-start | bytes 12582912 | tf_op jit(solution)/shard_map/all_to_all | solution.py:150
  238.5 3.3 collective-permute-done.10
  243.9 14.3 %all-reduce = (f32[]{:T(128)}, f32[]{:T(128)}) all-reduce(f32[]{:T(128)} %get-tuple-element.150, f32[]{:T(128)} %add_reduce_fusion), channel_id=1, replica_groups=mesh['mem'=4,'tile'=8] {'tile'}, use_global_device_ids=true, to_apply=%region_5.6 | all-reduce | flops 2 | bytes 16 | tf_op jit(solution)/shard_map/psum | solution.py:160
  259.5 7.0 %multiply_reduce_fusion = (f32[]{:T(128)}, f32[1024,1024]{1,0:T(8,128)}) fusion(f32[]{:T(128)S(6)} %div.46, f32[2048,256]{0,1:T(8,128)S(1)} %constant_dynamic-update-slice_fusion, s32[]{:T(128)S(6)} %select_n.54, f32[256]{0:T(256)S(1)} %get-tuple-element.151, f32[256]{0:T(256)S(1)} %get-tuple-element.6), kind=kOutput, calls=%fused_computation.12 | convolution fusion | flops 3225157632 | bytes 6296068 | tf_op jit(solution)/shard_map/mo,no->mn/dot_general | solution.py:96
  268.8 6.2 %fusion.191 = f32[1,1024]{1,0:T(1,128)S(1)} fusion(f32[1,1024]{1,0:T(1,128)S(1)} %fusion.183, f32[1024,1024]{1,0:T(8,128)} %get-tuple-element.158, f32[]{:T(128)S(6)} %div.49, f32[]{:T(128)S(6)} %div.46), kind=kOutput, calls=%fused_computation.299 | convolution fusion | flops 17825792 | bytes 4202504 | tf_op jit(solution)/shard_map/dot_general | solution.py:117
  275.1 3.9 fusion.189
  279.0 3.9 fusion.201
  283.0 4.1 fusion.200
  290.2 3.9 fusion.199
  294.1 3.9 fusion.187
  298.0 3.9 fusion.198
  302.0 4.3 fusion.197
  306.3 3.1 add_multiply_fusion.8
  310.3 3.1 reduce_sum.92
  313.4 6.6 %copy.18 = f32[4,256,1536]{2,1,0:T(8,128)} copy(f32[4,256,1536]{1,2,0:T(8,128)} %bitcast.30) | data formatting | bytes 12582912 | tf_op jit(solution)/shard_map/all_to_all | solution.py:150
  320.0 3.6 bitcast_subtract_fusion
  324.0 20.7 %fusion.203 = f32[1024,1536]{1,0:T(8,128)S(1)} fusion(f32[1024,1536]{1,0:T(8,128)S(1)} %bitcast_subtract_fusion, f32[1024,1024]{1,0:T(8,128)S(1)} %copy-done.1, f32[]{:T(128)S(6)} %div.49, f32[]{:T(128)S(6)} %div.46), kind=kOutput, calls=%fused_computation.329 | convolution fusion | flops 19332595712 | bytes 16777224 | tf_op jit(solution)/shard_map/dot_general | solution.py:117
  347.8 21.6 %multiply_subtract_fusion.1 = f32[1024,1536]{1,0:T(8,128)S(1)} fusion(f32[1024,1536]{1,0:T(8,128)S(1)} %bitcast_subtract_fusion, f32[1024,1536]{1,0:T(8,128)S(1)} %fusion.203, f32[1024,1024]{1,0:T(8,128)S(1)} %copy-done.1, f32[]{:T(128)S(6)} %div.49, f32[]{:T(128)S(6)} %div.46), kind=kOutput, calls=%fused_computation.9 | convolution fusion | flops 19335741440 | bytes 23068680 | tf_op jit(solution)/shard_map/dot_general | solution.py:120
  372.0 22.3 %fusion.202 = f32[1024,1536]{1,0:T(8,128)} fusion(f32[1024,1536]{1,0:T(8,128)S(1)} %multiply_subtract_fusion.1, f32[1024,1024]{1,0:T(8,128)S(1)} %copy-done.1, f32[]{:T(128)S(6)} %div.49, f32[]{:T(128)S(6)} %div.46), kind=kOutput, calls=%fused_computation.328 | convolution fusion | flops 19332595712 | bytes 16777224 | tf_op jit(solution)/shard_map/dot_general | solution.py:120
  394.3 32.6 %add_add_fusion = f32[1024,1536]{1,0:T(8,128)} fusion(f32[1024,1536]{1,0:T(8,128)} %copy-done.21, f32[1024,1536]{1,0:T(8,128)} %copy-done.20, f32[1024,1536]{1,0:T(8,128)S(1)} %bitcast_subtract_fusion, f32[1024,1536]{1,0:T(8,128)} %fusion.202, f32[1536]{0:T(1024)S(1)} %convolution_reduce_fusion, f32[]{:T(128)} %bitcast.35, f32[]{:T(128)} %bitcast.34, ...), kind=kOutput, calls=%fused_computation.7 | convolution fusion | flops 19360907264 | bytes 35663904 | tf_op jit(solution)/shard_map/dot_general | solution.py:120
  427.0 74.3 %all_to_all.35 = f32[4,256,1536]{2,1,0:T(8,128)S(1)} all-to-all(f32[4,256,1536]{2,1,0:T(8,128)} %bitcast.139), channel_id=1, replica_groups=mesh['mem'=4,'tile'=8] {'mem'}, dimensions={0} | all-to-all | bytes 12582912 | tf_op jit(solution)/shard_map/all_to_all | solution.py:164
  501.3 6.7 %copy.19 = f32[256,4,1536]{2,1,0:T(4,128)} copy(f32[256,4,1536]{2,0,1:T(8,128)S(1)} %bitcast.138) | data formatting | bytes 12582912 | tf_op jit(solution)/shard_map/all_to_all | solution.py:164
  507.9 8.3 %reshape.53 = f32[256,3,8,256]{3,2,1,0:T(8,128)} reshape(f32[256,4,1536]{2,1,0:T(4,128)} %copy.19) | data formatting | bytes 12582912 | tf_op jit(solution)/shard_map/reshape | solution.py:165
  (156 shorter events, 91.4 us)
Async XLA Ops:
  8.0 20.1 %collective-permute-start = (f32[256,3,1,256]{0,3,2,1:T(8,128)S(1)}, f32[256,3,1,256]{0,3,2,1:T(8,128)S(1)}, u32[]{:S(2)}, u32[]{:S(2)}) collective-permute-start(f32[256,3,1,256]{0,3,2,1:T(8,128)S(1)} %get-tuple-element.35), channel_id=1, source_target_pairs={{0,1},{1,2},{2,3},{3,4},{4,5},{5,6},{6,7},{7,0},{8,9},{9,10},{10,1... | collective-permute-start | bytes 2359304 | tf_op jit(solution)/shard_map/ppermute | solution.py:25
  8.6 20.0 %collective-permute-start.1 = (f32[256,3,1,256]{0,3,2,1:T(8,128)S(1)}, f32[256,3,1,256]{0,3,2,1:T(8,128)S(1)}, u32[]{:S(2)}, u32[]{:S(2)}) collective-permute-start(f32[256,3,1,256]{0,3,2,1:T(8,128)S(1)} %get-tuple-element.36), channel_id=1, source_target_pairs={{1,0},{2,1},{3,2},{4,3},{5,4},{6,5},{7,6},{0,7},{9,8},{10,9},{11,1... | collective-permute-start | bytes 2359304 | tf_op jit(solution)/shard_map/ppermute | solution.py:27
  48.3 5.0 copy-start.9
  48.3 5.0 copy-start.13
  53.3 3.8 copy-start.4
  53.3 3.8 copy-start.5
  53.3 4.6 copy-start.6
  53.3 5.2 copy-start.12
  63.2 18.8 %collective-permute-start.2 = (f32[256,3,1,256]{0,3,2,1:T(8,128)S(1)}, f32[256,3,1,256]{0,3,2,1:T(8,128)S(1)}, u32[]{:S(2)}, u32[]{:S(2)}) collective-permute-start(f32[256,3,1,256]{0,3,2,1:T(8,128)S(1)} %get-tuple-element.33), channel_id=1, source_target_pairs={{0,1},{1,2},{2,3},{3,4},{4,5},{5,6},{6,7},{7,0},{8,9},{9,10},{10,1... | collective-permute-start | bytes 2359304 | tf_op jit(solution)/shard_map/ppermute | solution.py:25
  65.3 17.3 %collective-permute-start.3 = (f32[256,3,1,256]{0,3,2,1:T(8,128)S(1)}, f32[256,3,1,256]{0,3,2,1:T(8,128)S(1)}, u32[]{:S(2)}, u32[]{:S(2)}) collective-permute-start(f32[256,3,1,256]{0,3,2,1:T(8,128)S(1)} %get-tuple-element.34), channel_id=1, source_target_pairs={{1,0},{2,1},{3,2},{4,3},{5,4},{6,5},{7,6},{0,7},{9,8},{10,9},{11,1... | collective-permute-start | bytes 2359304 | tf_op jit(solution)/shard_map/ppermute | solution.py:27
  98.1 4.7 copy-start.7
  106.9 5.6 %copy-start.2 = (f32[256,1,8,256]{0,3,2,1:T(8,128)}, f32[256,1,8,256]{0,3,2,1:T(8,128)S(1)}, u32[]{:S(2)}) copy-start(f32[256,1,8,256]{0,3,2,1:T(8,128)S(1)} %fusion.97) | copy-start | bytes 6291460
  112.5 1.8 copy-start.3
  114.4 18.8 %collective-permute-start.4 = (f32[256,3,1,256]{0,3,2,1:T(8,128)}, f32[256,3,1,256]{0,3,2,1:T(8,128)S(1)}, u32[]{:S(2)}, u32[]{:S(2)}) collective-permute-start(f32[256,3,1,256]{0,3,2,1:T(8,128)} %get-tuple-element.31), channel_id=1, source_target_pairs={{0,1},{1,2},{2,3},{3,4},{4,5},{5,6},{6,7},{7,0},{8,9},{9,10},{10,1... | collective-permute-start | bytes 2359304 | tf_op jit(solution)/shard_map/ppermute | solution.py:25
  116.8 17.6 %collective-permute-start.5 = (f32[256,3,1,256]{0,3,2,1:T(8,128)}, f32[256,3,1,256]{0,3,2,1:T(8,128)}, u32[]{:S(2)}, u32[]{:S(2)}) collective-permute-start(f32[256,3,1,256]{0,3,2,1:T(8,128)} %get-tuple-element.32), channel_id=1, source_target_pairs={{1,0},{2,1},{3,2},{4,3},{5,4},{6,5},{7,6},{0,7},{9,8},{10,9},{11,1... | collective-permute-start | bytes 2359304 | tf_op jit(solution)/shard_map/ppermute | solution.py:27
  150.5 4.6 copy-start.8
  163.6 4.3 copy-start.19
  163.6 4.3 copy-start.16
  163.8 18.4 %collective-permute-start.6 = (f32[256,3,1,256]{0,3,2,1:T(8,128)S(1)}, f32[256,3,1,256]{0,3,2,1:T(8,128)S(1)}, u32[]{:S(2)}, u32[]{:S(2)}) collective-permute-start(f32[256,3,1,256]{0,3,2,1:T(8,128)S(1)} %get-tuple-element.29), channel_id=1, source_target_pairs={{0,1},{1,2},{2,3},{3,4},{4,5},{5,6},{6,7},{7,0},{8,9},{9,10},{10,1... | collective-permute-start | bytes 2359304 | tf_op jit(solution)/shard_map/ppermute | solution.py:25
  165.8 17.3 %collective-permute-start.7 = (f32[256,3,1,256]{0,3,2,1:T(8,128)S(1)}, f32[256,3,1,256]{0,3,2,1:T(8,128)S(1)}, u32[]{:S(2)}, u32[]{:S(2)}) collective-permute-start(f32[256,3,1,256]{0,3,2,1:T(8,128)S(1)} %get-tuple-element.30), channel_id=1, source_target_pairs={{1,0},{2,1},{3,2},{4,3},{5,4},{6,5},{7,6},{0,7},{9,8},{10,9},{11,1... | collective-permute-start | bytes 2359304 | tf_op jit(solution)/shard_map/ppermute | solution.py:27
  167.9 15.2 %copy-start.17 = (pred[8]{0:T(512)(128)(4,1)}, pred[8]{0:T(512)(128)(4,1)S(1)}, u32[]{:S(2)}) copy-start(pred[8]{0:T(512)(128)(4,1)S(1)} %broadcast_compare_fusion) | copy-start | bytes 28
  199.6 4.0 copy-start.10
  203.6 3.4 copy-start.11
  210.2 22.9 %copy-start.14 = (f32[8,256]{1,0:T(8,128)S(1)}, f32[8,256]{1,0:T(8,128)}, u32[]{:S(2)}) copy-start(f32[8,256]{1,0:T(8,128)} %param.8) | copy-start | bytes 24580
  210.2 22.9 %copy-start.15 = (f32[8,256]{1,0:T(8,128)S(1)}, f32[8,256]{1,0:T(8,128)}, u32[]{:S(2)}) copy-start(f32[8,256]{1,0:T(8,128)} %param.9) | copy-start | bytes 24580
  210.3 22.9 %copy-start.18 = (pred[8]{0:T(512)(128)(4,1)S(1)}, pred[8]{0:T(512)(128)(4,1)}, u32[]{:S(2)}) copy-start(pred[8]{0:T(512)(128)(4,1)} %copy-done.17) | copy-start | bytes 28
  214.1 8.6 %collective-permute-start.8 = (f32[256,256]{0,1:T(8,128)S(1)}, f32[256,256]{0,1:T(8,128)S(1)}, u32[]{:S(2)}, u32[]{:S(2)}) collective-permute-start(f32[256,256]{0,1:T(8,128)S(1)} %select_bitcast_fusion), channel_id=1, source_target_pairs={{0,8},{8,16},{16,24},{24,0},{1,9},{9,17},{17,25},{25,1},{2,10},{10... | collective-permute-start | bytes 786440 | tf_op jit(solution)/shard_map/ppermute | solution.py:154
  222.7 9.7 %collective-permute-start.9 = (f32[256,256]{0,1:T(8,128)S(1)}, f32[256,256]{0,1:T(8,128)S(1)}, u32[]{:S(2)}, u32[]{:S(2)}) collective-permute-start(f32[256,256]{0,1:T(8,128)S(1)} %collective-permute-done.8), channel_id=1, source_target_pairs={{0,8},{8,16},{16,24},{24,0},{1,9},{9,17},{17,25},{25,1},{2,10},{10... | collective-permute-start | bytes 786440 | tf_op jit(solution)/shard_map/ppermute | solution.py:154
  232.4 9.4 %collective-permute-start.10 = (f32[256,256]{0,1:T(8,128)S(1)}, f32[256,256]{0,1:T(8,128)S(1)}, u32[]{:S(2)}, u32[]{:S(2)}) collective-permute-start(f32[256,256]{0,1:T(8,128)S(1)} %collective-permute-done.9), channel_id=1, source_target_pairs={{0,8},{8,16},{16,24},{24,0},{1,9},{9,17},{17,25},{25,1},{2,10},{10... | collective-permute-start | bytes 786440 | tf_op jit(solution)/shard_map/ppermute | solution.py:154
  233.2 77.0 %all-to-all-start = ((f32[256,4,1536]{0,2,1:T(8,128)}), f32[256,4,1536]{0,2,1:T(8,128)}, u32[]{:S(2)}, u32[]{:S(2)}) async-start(f32[256,4,1536]{0,2,1:T(8,128)} %bitcast.137), calls=%async_computation | async-start | bytes 12582912 | tf_op jit(solution)/shard_map/all_to_all | solution.py:150
  268.8 6.3 %copy-start = (f32[1024,1024]{1,0:T(8,128)S(1)}, f32[1024,1024]{1,0:T(8,128)}, u32[]{:S(2)}) copy-start(f32[1024,1024]{1,0:T(8,128)} %get-tuple-element.158) | copy-start | bytes 12582916
  320.0 4.0 copy-start.1
  344.7 3.1 copy-start.20
  369.3 2.7 copy-start.21
